TPU v7x, 256 devices: a whole 4x4x8 slice. The times are simulated.
256 devices in a mesh: job: 4 (over y), zero: 16 (over z, core), cols: 4 (over x).
Axes of the slice: x: 4, y: 4, z: 8, core: 2. Of those that a mesh axis runs over, the one named last changes fastest.
Arguments:
- weight_query: bfloat16 [12288, 3072], P(('job', 'zero'), 'cols'), parts along dimension 0, may hold values from -0.109375 to 0.109375
- low_query: bfloat16 [12288, 32], P(('job', 'zero')), parts along dimension 0, may hold values from -0.109375 to 0.109375
- high_query: bfloat16 [128, 3072], P('job', 'cols'), parts along dimension 0, may hold values from -1 to 1
- weight_key: bfloat16 [12288, 1024], P(('job', 'zero'), 'cols'), parts along dimension 0, may hold values from -0.109375 to 0.109375
- low_key: bfloat16 [12288, 32], P(('job', 'zero')), parts along dimension 0, may hold values from -0.109375 to 0.109375
- high_key: bfloat16 [128, 1024], P('job', 'cols'), parts along dimension 0, may hold values from -1 to 1
- weight_value: bfloat16 [12288, 1024], P(('job', 'zero'), 'cols'), parts along dimension 0, may hold values from -0.109375 to 0.109375
- low_value: bfloat16 [12288, 32], P(('job', 'zero')), parts along dimension 0, may hold values from -0.109375 to 0.109375
- high_value: bfloat16 [128, 1024], P('job', 'cols'), parts along dimension 0, may hold values from -1 to 1
- weight_mixed: bfloat16 [12288, 3072], P(('job', 'cols'), 'zero'), parts along dimension 0, may hold values from -0.109375 to 0.109375
- low_mixed: bfloat16 [12288, 32], P(('job', 'cols')), parts along dimension 0, may hold values from -0.109375 to 0.109375
- high_mixed: bfloat16 [128, 3072], P('job', 'zero'), parts along dimension 0, may hold values from -1 to 1
- norm_train: float32 [12288], P(('job', 'zero', 'cols')), parts along dimension 0, may hold values from 0.25 to 1.75
- norm_step: float32 [12288], P(('job', 'zero', 'cols')), parts along dimension 0, may hold values from -0.3 to 0.3
Outputs:
- serving_query: bfloat16 [12288, 3072], P('job', 'cols'), parts along dimension 0
- serving_key: bfloat16 [12288, 1024], P('job', 'cols'), parts along dimension 0
- serving_value: bfloat16 [12288, 1024], P('job', 'cols'), parts along dimension 0
- serving_mixed: bfloat16 [12288, 3072], P(('job', 'cols')), parts along dimension 0
- serve_norm: bfloat16 [12288], P('job'), parts along dimension 0
There are 4 independent parts, one for each index of `job`. A program takes and returns all parts, laid end to end along the dimension named above; each array names one. Nothing has to cross between parts.
All inputs are finite; a program needn't handle non-finite values.
Results may differ from a plain program's by a relative error of at most 0.001.
Values may be sent and summed in bfloat16 or wider, within the bound.
A program may use at most 128 MiB of HBM per device.

v0:
```python
import jax
import jax.numpy as jnp
from jax import lax
from jax.sharding import PartitionSpec as P

mix_rate = 2.0


def gather_turned(arrays, axis, dims):
    turned = [jnp.moveaxis(a, dim, 0) for a, dim in zip(arrays, dims)]
    widths = [t[0].size for t in turned]
    both = jnp.concatenate([t.reshape(-1, w) for t, w in zip(turned, widths)], axis=1)
    whole = lax.all_gather(both, axis, axis=0, tiled=True)
    tiles = jnp.split(whole, [sum(widths[:k]) for k in range(1, len(widths))], axis=1)
    return tuple(
        (
            jnp.moveaxis(b.reshape(-1, *t.shape[1:]), 0, dim)
            for b, t, dim in zip(tiles, turned, dims)
        )
    )


def sent_to_all(array, axis):
    copies = jnp.broadcast_to(array, (lax.axis_size(axis), *array.shape))
    return lax.all_to_all(copies, axis, split_axis=0, concat_axis=0, tiled=True)


def joined_along(tiles, dim):
    tiles = jnp.moveaxis(tiles, 0, dim)
    dims = tiles.shape
    return tiles.reshape(*dims[:dim], dims[dim] * dims[dim + 1], *dims[dim + 2 :])


def collect(array, axis, dim):
    tiles = sent_to_all(array, axis)
    return joined_along(tiles, dim)


def on_device(
    weight_query,
    low_query,
    high_query,
    weight_key,
    low_key,
    high_key,
    weight_value,
    low_value,
    high_value,
    weight_mixed,
    low_mixed,
    high_mixed,
    norm_train,
    norm_step,
):
    whole_query = weight_query.astype(jnp.float32) + mix_rate * jnp.dot(
        low_query, high_query, preferred_element_type=jnp.float32
    )
    whole_key = weight_key.astype(jnp.float32) + mix_rate * jnp.dot(
        low_key, high_key, preferred_element_type=jnp.float32
    )
    whole_value = weight_value.astype(jnp.float32) + mix_rate * jnp.dot(
        low_value, high_value, preferred_element_type=jnp.float32
    )
    whole_mixed = weight_mixed.astype(jnp.float32) + mix_rate * jnp.dot(
        low_mixed, high_mixed, preferred_element_type=jnp.float32
    )
    narrow_query, narrow_key, narrow_value, narrow_mixed = (
        whole_query.astype(jnp.bfloat16),
        whole_key.astype(jnp.bfloat16),
        whole_value.astype(jnp.bfloat16),
        whole_mixed.astype(jnp.bfloat16),
    )
    serving_query, serving_key, serving_value, serving_mixed = gather_turned(
        (narrow_query, narrow_key, narrow_value, narrow_mixed), "zero", (0, 0, 0, 1)
    )
    serve_norm = collect((norm_train + norm_step).astype(jnp.bfloat16), ("zero", "cols"), 0)
    return (serving_query, serving_key, serving_value, serving_mixed, serve_norm)


def solution(mesh):
    placed = (
        P(("job", "zero"), "cols"),
        P(("job", "zero"), None),
        P("job", "cols"),
        P(("job", "zero"), "cols"),
        P(("job", "zero"), None),
        P("job", "cols"),
        P(("job", "zero"), "cols"),
        P(("job", "zero"), None),
        P("job", "cols"),
        P(("job", "cols"), "zero"),
        P(("job", "cols"), None),
        P("job", "zero"),
        P(("job", "zero", "cols")),
        P(("job", "zero", "cols")),
    )
    return jax.shard_map(
        on_device,
        mesh=mesh,
        in_specs=placed,
        out_specs=(
            P("job", "cols"),
            P("job", "cols"),
            P("job", "cols"),
            P(("job", "cols"), None),
            P("job"),
        ),
        check_vma=False,
    )
```

profile of v0, /device:TPU:1, one launch (start us, length us, event | category | flops | bytes accessed | tf_op | source)
XLA Modules:
  0.0 119.2 jit_solution(13461833786214713967)
XLA Ops:
  7.2 0.0 copy-start
  7.2 0.0 all-gather.2.cloned.1.call-start
  7.2 0.7 copy-done
  8.0 1.3 %fusion.4 = bf16[192,768]{1,0:T(8,128)(2,1)S(1)} fusion(bf16[768,32]{0,1:T(8,128)(2,1)S(1)} %copy-done, bf16[32,192]{1,0:T(8,128)(2,1)} %param.25, bf16[768,192]{0,1:T(8,128)(2,1)} %param.23), kind=kOutput, calls=%fused_computation.7 | convolution fusion | flops 10027008 | bytes 651264 | tf_op jit(solution)/shard_map/dot_general | solution.py:64
  9.2 1.1 fusion.8
  10.4 0.0 copy-start.1
  10.4 0.0 copy-start.2
  10.4 1.1 fusion.7
  11.6 1.3 %fusion.2 = bf16[192,768]{1,0:T(8,128)(2,1)S(1)} fusion(bf16[192,32]{0,1:T(8,128)(2,1)} %param.15, bf16[32,768]{1,0:T(8,128)(2,1)} %param.16, bf16[192,768]{1,0:T(8,128)(2,1)} %param.14), kind=kOutput, calls=%fused_computation.5 | convolution fusion | flops 10027008 | bytes 651264 | tf_op jit(solution)/shard_map/dot_general | solution.py:55
  12.8 1.0 pad_maximum_fusion
  13.8 0.0 all-gather.2.cloned.1.call-update
  13.8 0.0 copy-done.1
  13.8 0.0 copy-done.2
  13.9 22.0 %all_to_all.6 = bf16[64,1,48]{2,1,0:T(2,128)(2,1)S(1)} all-to-all(bf16[64,1,48]{2,1,0:T(2,128)(2,1)S(1)} %broadcast_in_dim.3), channel_id=1, replica_groups=mesh['job'=4,'zero'=16,'cols'=4] {'zero','cols'}, dimensions={0} | all-to-all | bytes 12288 | tf_op jit(solution)/shard_map/all_to_all | solution.py:25
  35.8 0.1 reduce
  35.9 0.7 reshape.18
  36.6 57.3 %all-gather.2.cloned.1.call-done = bf16[3072,2048]{1,0:T(8,128)(2,1)} async-done(((bf16[192,2048]{1,0:T(8,128)(2,1)}), bf16[3072,2048]{1,0:T(8,128)(2,1)}) %all-gather.2.cloned.1.call-update) | async-done | bytes 12582928 | tf_op jit(solution)/shard_map/all_gather | solution.py:13
  93.9 8.1 %slice_bitcast_fusion = (bf16[768,3072]{0,1:T(8,128)(2,1)}, bf16[3072,768]{1,0:T(8,128)(2,1)}) fusion(bf16[3072,2048]{1,0:T(8,128)(2,1)} %all-gather.2.cloned.1.call-done), kind=kLoop, calls=%fused_computation | loop fusion | bytes 18874368 | tf_op jit(solution)/shard_map/transpose | solution.py:17
  102.0 6.6 %copy.21 = bf16[768,3072]{1,0:T(8,128)(2,1)} copy(bf16[768,3072]{0,1:T(8,128)(2,1)} %get-tuple-element.20) | data formatting | bytes 9437184
  108.6 3.8 %fusion.9 = (bf16[3072,256]{1,0:T(8,128)(2,1)}, bf16[3072,256]{1,0:T(8,128)(2,1)}) fusion(bf16[3072,2048]{1,0:T(8,128)(2,1)} %all-gather.2.cloned.1.call-done), kind=kLoop, calls=%fused_computation.16 | loop fusion | bytes 6291456 | tf_op jit(solution)/shard_map/split | solution.py:14
  (2 shorter events, 0.0 us)
Async XLA Ops:
  7.2 0.8 copy-start
  7.2 86.7 %all-gather.2.cloned.1.call-start = ((), (), s32[]{:S(2)}) async-start(), calls=%async_computation.1 | async-start | bytes 13369344 | tf_op jit(solution)/shard_map/all_gather | solution.py:13
  10.4 3.4 %copy-start.1 = (f32[48]{0:T(128)S(1)}, f32[48]{0:T(128)}, u32[]{:S(2)}) copy-start(f32[48]{0:T(128)} %param.26) | copy-start | bytes 580
  10.4 3.4 %copy-start.2 = (f32[48]{0:T(128)S(1)}, f32[48]{0:T(128)}, u32[]{:S(2)}) copy-start(f32[48]{0:T(128)} %param.27) | copy-start | bytes 580
Sparse Core Ops, SparseCore 0:
  13.9 79.9 all-gather.1
where the time goes:
time: 120 us; the launch traced here: 119 us
  waiting for transfers between devices  57.3 us (48%)
  blocking collectives  22 us (18%)
  local copies, waits for them, and re-layouts  20 us (17%)
  between operations  14.1 us (12%)
  matrix products  4.81 us (4%)
    all_gather x1, waiting for transfers between devices, gather_turned(): whole = lax.all_gather(both, axis, axis=0, tiled=True)  57.3 us
    all_to_all x1, blocking collectives, sent_to_all(): return lax.all_to_all(copies, axis, split_axis=0, concat_axis=0, tiled=True)  22 us
    transpose x1, local copies, waits for them, and re-layouts, gather_turned(): jnp.moveaxis(b.reshape(-1, *t.shape[1:]), 0, dim)  8.13 us
    unnamed x7, local copies, waits for them, and re-layouts  7.37 us
    split x1, local copies, waits for them, and re-layouts, gather_turned(): jnp.split(whole, [sum(widths[:k]) for k in range(1, len(widths))], axis=1)  3.76 us
  transfers between devices with their start and end apart: 1, of which 1 were waited for; matrix products, arithmetic and copies ran while one was open for 1% of the time, Pallas kernels for 0%

commit v1 on v0

--- a/solution.py
+++ b/solution.py
@@ -10,7 +10,10 @@
     turned = [jnp.moveaxis(a, dim, 0) for a, dim in zip(arrays, dims)]
     widths = [t[0].size for t in turned]
     both = jnp.concatenate([t.reshape(-1, w) for t, w in zip(turned, widths)], axis=1)
-    whole = lax.all_gather(both, axis, axis=0, tiled=True)
+    size = lax.axis_size(axis)
+    blocks = jnp.stack([both for _ in range(size)])
+    blocks = lax.all_to_all(blocks, axis, split_axis=0, concat_axis=0)
+    whole = jnp.concatenate(blocks, axis=0)
     tiles = jnp.split(whole, [sum(widths[:k]) for k in range(1, len(widths))], axis=1)
     return tuple(
         (

time: 120 us -> 328 us (2.73)
  waiting for transfers between devices: 57.3 us -> 277 us
  blocking collectives: 22 us -> 0 us
  starting transfers between devices: 0.04 us -> 18.6 us
  between operations: 14.1 us -> 0.69 us
  local copies, waits for them, and re-layouts: 20 us -> 25.9 us
    all_to_all x0 -> x2, waiting for transfers between devices: none -> 277 us  [the longest x1 273 us: gather_turned(): blocks = lax.all_to_all(blocks, axis, split_axis=0, concat_axis=0)]
    all_gather x1 -> x0, waiting for transfers between devices: 57.3 us -> none  [gather_turned(): whole = lax.all_gather(both, axis, axis=0, tiled=True)]
    all_to_all x1 -> x0, blocking collectives: 22 us -> none  [sent_to_all(): return lax.all_to_all(copies, axis, split_axis=0, concat_axis=0, tiled=True)]
    all_to_all x0 -> x2, starting transfers between devices: none -> 18.6 us  [the longest x1 13 us: sent_to_all(): return lax.all_to_all(copies, axis, split_axis=0, concat_axis=0, tiled=True)]
    another operation x0 -> x1, local copies, waits for them, and re-layouts: none -> 6.07 us  [gather_turned(): blocks = jnp.stack([both for _ in range(size)])]
    unnamed x7 -> x3, local copies, waits for them, and re-layouts: 7.37 us -> 6.62 us
  transfers between devices with their start and end apart: 1 -> 2, of which waited for: 1 -> 2; matrix products, arithmetic and copies ran while one was open for 1% -> 2% of each run, Pallas kernels for 0% -> 0%
where the time goes in v1:
time: 328 us
  waiting for transfers between devices  277 us (84%)
  local copies, waits for them, and re-layouts  25.9 us (8%)
  starting transfers between devices  18.6 us (6%)
  matrix products  4.81 us (1%)
    all_to_all x1, waiting for transfers between devices, gather_turned(): blocks = lax.all_to_all(blocks, axis, split_axis=0, concat_axis=0)  273 us
    all_to_all x1, starting transfers between devices, sent_to_all(): return lax.all_to_all(copies, axis, split_axis=0, concat_axis=0, tiled=True)  13 us
    transpose x1, local copies, waits for them, and re-layouts, gather_turned(): jnp.moveaxis(b.reshape(-1, *t.shape[1:]), 0, dim)  8.13 us
    unnamed x3, local copies, waits for them, and re-layouts  6.62 us
  transfers between devices with their start and end apart: 2, of which 2 were waited for; matrix products, arithmetic and copies ran while one was open for 2% of the time, Pallas kernels for 0%

profile of v1, /device:TPU:1, one launch (start us, length us, event | category | flops | bytes accessed | tf_op | source)
XLA Modules:
  0.0 327.6 jit_solution(16704601228298147631)
XLA Ops:
  0.6 0.0 copy-start
  0.6 0.7 add_convert_fusion
  1.3 0.6 broadcast_in_dim.3
  2.0 13.0 %all-to-all-start.1 = ((bf16[64,1,48]{2,1,0:T(2,128)(2,1)}), bf16[64,1,48]{2,1,0:T(2,128)(2,1)S(1)}, u32[]{:S(2)}, u32[]{:S(2)}) async-start(bf16[64,1,48]{2,1,0:T(2,128)(2,1)} %broadcast_in_dim.3), calls=%async_computation.1 | async-start | bytes 65536 | tf_op jit(solution)/shard_map/all_to_all | solution.py:28
  15.0 0.0 copy-done
  15.0 1.3 fusion.4
  16.2 1.1 fusion.8
  17.4 1.1 fusion.7
  18.5 1.3 fusion.2
  19.8 0.1 pad_maximum_fusion
  19.9 4.2 %all-to-all-done.1 = bf16[64,1,48]{2,1,0:T(2,128)(2,1)S(1)} async-done(((bf16[64,1,48]{2,1,0:T(2,128)(2,1)}), bf16[64,1,48]{2,1,0:T(2,128)(2,1)S(1)}, u32[]{:S(2)}, u32[]{:S(2)}) %all-to-all-start.1) | async-done | bytes 6176 | tf_op jit(solution)/shard_map/all_to_all | solution.py:28
  24.1 6.1 %stack.2 = bf16[16,192,2048]{2,1,0:T(8,128)(2,1)} broadcast(bf16[192,2048]{1,0:T(8,128)(2,1)S(1)} %pad_maximum_fusion), dimensions={1,2} | broadcast | bytes 13369344 | tf_op jit(solution)/shard_map/stack | solution.py:14
  30.1 5.6 %all-to-all-start = ((bf16[16,192,2048]{2,1,0:T(8,128)(2,1)}), bf16[16,192,2048]{2,1,0:T(8,128)(2,1)}, u32[]{:S(2)}, u32[]{:S(2)}) async-start(bf16[16,192,2048]{2,1,0:T(8,128)(2,1)} %stack.2), calls=%async_computation | async-start | bytes 25165824 | tf_op jit(solution)/shard_map/all_to_all | solution.py:15
  35.8 0.1 reduce
  35.8 0.7 reshape.24
  36.5 272.5 %all-to-all-done = bf16[16,192,2048]{2,1,0:T(8,128)(2,1)} async-done(((bf16[16,192,2048]{2,1,0:T(8,128)(2,1)}), bf16[16,192,2048]{2,1,0:T(8,128)(2,1)}, u32[]{:S(2)}, u32[]{:S(2)}) %all-to-all-start) | async-done | bytes 12582944 | tf_op jit(solution)/shard_map/all_to_all | solution.py:15
  309.1 8.1 %slice_bitcast_fusion = (bf16[768,3072]{0,1:T(8,128)(2,1)}, bf16[3072,768]{1,0:T(8,128)(2,1)}) fusion(bf16[3072,2048]{1,0:T(8,128)(2,1)} %bitcast.1), kind=kLoop, calls=%fused_computation | loop fusion | bytes 18874368 | tf_op jit(solution)/shard_map/transpose | solution.py:20
  317.2 3.8 %fusion.9 = (bf16[3072,256]{1,0:T(8,128)(2,1)}, bf16[3072,256]{1,0:T(8,128)(2,1)}) fusion(bf16[3072,2048]{1,0:T(8,128)(2,1)} %bitcast.1), kind=kLoop, calls=%fused_computation.16 | loop fusion | bytes 6291456 | tf_op jit(solution)/shard_map/split | solution.py:17
  321.0 6.6 %copy.24 = bf16[768,3072]{1,0:T(8,128)(2,1)} copy(bf16[768,3072]{0,1:T(8,128)(2,1)} %get-tuple-element.20) | data formatting | bytes 9437184
Async XLA Ops:
  0.6 14.3 %copy-start = (bf16[768,32]{0,1:T(8,128)(2,1)S(1)}, bf16[768,32]{0,1:T(8,128)(2,1)}, u32[]{:S(2)}) copy-start(bf16[768,32]{0,1:T(8,128)(2,1)} %param.24) | copy-start | bytes 147460
  2.0 22.1 %all-to-all-start.1 = ((bf16[64,1,48]{2,1,0:T(2,128)(2,1)}), bf16[64,1,48]{2,1,0:T(2,128)(2,1)S(1)}, u32[]{:S(2)}, u32[]{:S(2)}) async-start(bf16[64,1,48]{2,1,0:T(2,128)(2,1)} %broadcast_in_dim.3), calls=%async_computation.1 | async-start | bytes 65536 | tf_op jit(solution)/shard_map/all_to_all | solution.py:28
  30.1 278.9 %all-to-all-start = ((bf16[16,192,2048]{2,1,0:T(8,128)(2,1)}), bf16[16,192,2048]{2,1,0:T(8,128)(2,1)}, u32[]{:S(2)}, u32[]{:S(2)}) async-start(bf16[16,192,2048]{2,1,0:T(8,128)(2,1)} %stack.2), calls=%async_computation | async-start | bytes 25165824 | tf_op jit(solution)/shard_map/all_to_all | solution.py:15
